TPU v7x, 32 devices: a 4x4x1 block of a 4x4x8 slice. The times are simulated.
32 devices in a mesh: dp: 1 (over z), col: 4 (over y), row: 8 (over x, core).
Axes of the slice: x: 4, y: 4, z: 1, core: 2. Of those that a mesh axis runs over, the one named last changes fastest.
The devices are a block of a 4x4x8 slice.
Arguments:
- a_mat: bfloat16 [16384, 3072], P(('dp', 'row'), 'col')
- b_mat: bfloat16 [3072, 8192], P('row', 'col')
Outputs:
- output: bfloat16 [16384, 8192], P(('dp', 'row'), 'col')
All inputs are finite; a program needn't handle non-finite values.
Results may differ from a plain program's by a relative error of at most 0.001.
Values are sent between devices in bfloat16 or wider.
A program may use at most 768 MiB of HBM per device.

v0:
```python
import jax
import jax.numpy as jnp
from jax import lax
from jax.sharding import PartitionSpec as P


def solution(mesh):
    num_rows = mesh.shape["row"]
    num_cols = mesh.shape["col"]
    num_steps = max(num_rows, num_cols)
    per_col = num_steps // num_cols
    per_row = num_steps // num_rows

    def local_product(a_blk, b_blk):
        row_id = lax.axis_index("row")
        col_id = lax.axis_index("col")
        panel_width = a_blk.shape[1] // per_col

        def update_step(k_step, c_accum):
            a_src = lax.dynamic_slice_in_dim(a_blk, (k_step % per_col) * panel_width, panel_width, axis=1)
            a_panel = lax.psum(jnp.where(col_id == k_step // per_col, a_src, jnp.zeros_like(a_src)), "col")
            b_src = lax.dynamic_slice_in_dim(b_blk, (k_step % per_row) * panel_width, panel_width, axis=0)
            b_panel = lax.psum(jnp.where(row_id == k_step // per_row, b_src, jnp.zeros_like(b_src)), "row")
            return c_accum + jnp.dot(a_panel, b_panel, preferred_element_type=jnp.float32)

        c_init = jnp.zeros((a_blk.shape[0], b_blk.shape[1]), jnp.float32)
        c_accum = lax.fori_loop(0, num_steps, update_step, c_init)
        return c_accum.astype(jnp.bfloat16)

    return jax.shard_map(local_product, mesh=mesh, in_specs=(P(("dp", "row"), "col"), P("row", "col")), out_specs=P(("dp", "row"), "col"), check_vma=False)
```

profile of v0, /device:TPU:97, one launch (start us, length us, event | category | flops | bytes accessed | tf_op | source)
XLA Modules:
  0.0 1029.2 jit_solution(10387047348848344328)
XLA Ops:
  6.5 1007.1 %while.17 = (s32[]{:T(128)}, f32[2048,2048]{1,0:T(8,128)}, s32[]{:T(128)}, bf16[2048,768]{1,0:T(8,128)(2,1)}, s32[]{:T(128)}, /*index=5*/bf16[384,2048]{1,0:T(8,...) while((s32[]{:T(128)}, f32[2048,2048]{1,0:T(8,128)}, ...), condition=%wide.region_3.4_spmd.clone, body=%wide.region_0.3_spmd.clone.sunk | while | flops 3232759808 | bytes 74449312 | solution.py:27
  6.6 1.3 broadcast_select_fusion.2
  8.0 1.0 copy-done
  9.0 1.4 dynamic-slice_select_fusion.2
  10.5 60.0 %all-reduce.5.cloned.1.call-done = bf16[384,2048]{1,0:T(8,128)(2,1)} async-done(((bf16[384,2048]{1,0:T(8,128)(2,1)}), bf16[384,2048]{1,0:T(8,128)(2,1)}) %all-reduce.5.cloned.1.call-update) | async-done | bytes 1572880 | tf_op jit(solution)/shard_map/while/body/eval_jaxpr/psum | solution.py:23
  70.5 49.2 %all-reduce.3.cloned.1.call-done = bf16[2048,384]{1,0:T(8,128)(2,1)} async-done(((bf16[2048,384]{1,0:T(8,128)(2,1)}), bf16[2048,384]{1,0:T(8,128)(2,1)}) %all-reduce.3.cloned.1.call-update) | async-done | bytes 1572880 | tf_op jit(solution)/shard_map/while/body/eval_jaxpr/psum | solution.py:21
  119.7 12.1 %select_add_fusion.2 = f32[2048,2048]{1,0:T(8,128)} fusion(f32[2048,2048]{1,0:T(8,128)} %get-tuple-element.276, pred[]{:T(512)S(6)} %compare.21, bf16[2048,384]{1,0:T(8,128)(2,1)} %all-reduce.3.cloned.1.call-done, bf16[384,2048]{1,0:T(8,128)(2,1)} %all-reduce.5.cloned.1.call-done), kind=kOutput, calls=%fused_computation.clone.1 | convolution fusion | flops 3229614080 | bytes 36700160 | tf_op jit(solution)/shard_map/while/body/eval_jaxpr/dot_general | solution.py:24
  131.9 2.8 broadcast_select_fusion.2
  134.9 1.4 dynamic-slice_select_fusion.2
  136.4 55.5 %all-reduce.5.cloned.1.call-done = bf16[384,2048]{1,0:T(8,128)(2,1)} async-done(((bf16[384,2048]{1,0:T(8,128)(2,1)}), bf16[384,2048]{1,0:T(8,128)(2,1)}) %all-reduce.5.cloned.1.call-update) | async-done | bytes 1572880 | tf_op jit(solution)/shard_map/while/body/eval_jaxpr/psum | solution.py:23
  191.9 49.0 %all-reduce.3.cloned.1.call-done = bf16[2048,384]{1,0:T(8,128)(2,1)} async-done(((bf16[2048,384]{1,0:T(8,128)(2,1)}), bf16[2048,384]{1,0:T(8,128)(2,1)}) %all-reduce.3.cloned.1.call-update) | async-done | bytes 1572880 | tf_op jit(solution)/shard_map/while/body/eval_jaxpr/psum | solution.py:21
  240.9 17.0 %select_add_fusion.2 = f32[2048,2048]{1,0:T(8,128)} fusion(f32[2048,2048]{1,0:T(8,128)} %get-tuple-element.276, pred[]{:T(512)S(6)} %compare.21, bf16[2048,384]{1,0:T(8,128)(2,1)} %all-reduce.3.cloned.1.call-done, bf16[384,2048]{1,0:T(8,128)(2,1)} %all-reduce.5.cloned.1.call-done), kind=kOutput, calls=%fused_computation.clone.1 | convolution fusion | flops 3229614080 | bytes 36700160 | tf_op jit(solution)/shard_map/while/body/eval_jaxpr/dot_general | solution.py:24
  257.9 1.3 broadcast_select_fusion.2
  259.3 1.0 copy-done
  260.4 1.4 dynamic-slice_select_fusion.2
  261.9 55.7 %all-reduce.5.cloned.1.call-done = bf16[384,2048]{1,0:T(8,128)(2,1)} async-done(((bf16[384,2048]{1,0:T(8,128)(2,1)}), bf16[384,2048]{1,0:T(8,128)(2,1)}) %all-reduce.5.cloned.1.call-update) | async-done | bytes 1572880 | tf_op jit(solution)/shard_map/while/body/eval_jaxpr/psum | solution.py:23
  317.6 49.0 %all-reduce.3.cloned.1.call-done = bf16[2048,384]{1,0:T(8,128)(2,1)} async-done(((bf16[2048,384]{1,0:T(8,128)(2,1)}), bf16[2048,384]{1,0:T(8,128)(2,1)}) %all-reduce.3.cloned.1.call-update) | async-done | bytes 1572880 | tf_op jit(solution)/shard_map/while/body/eval_jaxpr/psum | solution.py:21
  366.6 17.0 %select_add_fusion.2 = f32[2048,2048]{1,0:T(8,128)} fusion(f32[2048,2048]{1,0:T(8,128)} %get-tuple-element.276, pred[]{:T(512)S(6)} %compare.21, bf16[2048,384]{1,0:T(8,128)(2,1)} %all-reduce.3.cloned.1.call-done, bf16[384,2048]{1,0:T(8,128)(2,1)} %all-reduce.5.cloned.1.call-done), kind=kOutput, calls=%fused_computation.clone.1 | convolution fusion | flops 3229614080 | bytes 36700160 | tf_op jit(solution)/shard_map/while/body/eval_jaxpr/dot_general | solution.py:24
  383.6 1.3 broadcast_select_fusion.2
  385.1 1.0 copy-done
  386.1 1.4 dynamic-slice_select_fusion.2
  387.6 56.0 %all-reduce.5.cloned.1.call-done = bf16[384,2048]{1,0:T(8,128)(2,1)} async-done(((bf16[384,2048]{1,0:T(8,128)(2,1)}), bf16[384,2048]{1,0:T(8,128)(2,1)}) %all-reduce.5.cloned.1.call-update) | async-done | bytes 1572880 | tf_op jit(solution)/shard_map/while/body/eval_jaxpr/psum | solution.py:23
  443.6 49.2 %all-reduce.3.cloned.1.call-done = bf16[2048,384]{1,0:T(8,128)(2,1)} async-done(((bf16[2048,384]{1,0:T(8,128)(2,1)}), bf16[2048,384]{1,0:T(8,128)(2,1)}) %all-reduce.3.cloned.1.call-update) | async-done | bytes 1572880 | tf_op jit(solution)/shard_map/while/body/eval_jaxpr/psum | solution.py:21
  492.8 17.0 %select_add_fusion.2 = f32[2048,2048]{1,0:T(8,128)} fusion(f32[2048,2048]{1,0:T(8,128)} %get-tuple-element.276, pred[]{:T(512)S(6)} %compare.21, bf16[2048,384]{1,0:T(8,128)(2,1)} %all-reduce.3.cloned.1.call-done, bf16[384,2048]{1,0:T(8,128)(2,1)} %all-reduce.5.cloned.1.call-done), kind=kOutput, calls=%fused_computation.clone.1 | convolution fusion | flops 3229614080 | bytes 36700160 | tf_op jit(solution)/shard_map/while/body/eval_jaxpr/dot_general | solution.py:24
  509.8 1.3 broadcast_select_fusion.2
  511.2 1.0 copy-done
  512.3 1.4 dynamic-slice_select_fusion.2
  513.8 56.0 %all-reduce.5.cloned.1.call-done = bf16[384,2048]{1,0:T(8,128)(2,1)} async-done(((bf16[384,2048]{1,0:T(8,128)(2,1)}), bf16[384,2048]{1,0:T(8,128)(2,1)}) %all-reduce.5.cloned.1.call-update) | async-done | bytes 1572880 | tf_op jit(solution)/shard_map/while/body/eval_jaxpr/psum | solution.py:23
  569.8 49.0 %all-reduce.3.cloned.1.call-done = bf16[2048,384]{1,0:T(8,128)(2,1)} async-done(((bf16[2048,384]{1,0:T(8,128)(2,1)}), bf16[2048,384]{1,0:T(8,128)(2,1)}) %all-reduce.3.cloned.1.call-update) | async-done | bytes 1572880 | tf_op jit(solution)/shard_map/while/body/eval_jaxpr/psum | solution.py:21
  618.9 17.0 %select_add_fusion.2 = f32[2048,2048]{1,0:T(8,128)} fusion(f32[2048,2048]{1,0:T(8,128)} %get-tuple-element.276, pred[]{:T(512)S(6)} %compare.21, bf16[2048,384]{1,0:T(8,128)(2,1)} %all-reduce.3.cloned.1.call-done, bf16[384,2048]{1,0:T(8,128)(2,1)} %all-reduce.5.cloned.1.call-done), kind=kOutput, calls=%fused_computation.clone.1 | convolution fusion | flops 3229614080 | bytes 36700160 | tf_op jit(solution)/shard_map/while/body/eval_jaxpr/dot_general | solution.py:24
  635.8 1.3 broadcast_select_fusion.2
  637.3 1.0 copy-done
  638.3 1.4 dynamic-slice_select_fusion.2
  639.8 56.0 %all-reduce.5.cloned.1.call-done = bf16[384,2048]{1,0:T(8,128)(2,1)} async-done(((bf16[384,2048]{1,0:T(8,128)(2,1)}), bf16[384,2048]{1,0:T(8,128)(2,1)}) %all-reduce.5.cloned.1.call-update) | async-done | bytes 1572880 | tf_op jit(solution)/shard_map/while/body/eval_jaxpr/psum | solution.py:23
  695.8 49.0 %all-reduce.3.cloned.1.call-done = bf16[2048,384]{1,0:T(8,128)(2,1)} async-done(((bf16[2048,384]{1,0:T(8,128)(2,1)}), bf16[2048,384]{1,0:T(8,128)(2,1)}) %all-reduce.3.cloned.1.call-update) | async-done | bytes 1572880 | tf_op jit(solution)/shard_map/while/body/eval_jaxpr/psum | solution.py:21
  744.9 17.0 %select_add_fusion.2 = f32[2048,2048]{1,0:T(8,128)} fusion(f32[2048,2048]{1,0:T(8,128)} %get-tuple-element.276, pred[]{:T(512)S(6)} %compare.21, bf16[2048,384]{1,0:T(8,128)(2,1)} %all-reduce.3.cloned.1.call-done, bf16[384,2048]{1,0:T(8,128)(2,1)} %all-reduce.5.cloned.1.call-done), kind=kOutput, calls=%fused_computation.clone.1 | convolution fusion | flops 3229614080 | bytes 36700160 | tf_op jit(solution)/shard_map/while/body/eval_jaxpr/dot_general | solution.py:24
  761.9 1.3 broadcast_select_fusion.2
  764.3 1.4 dynamic-slice_select_fusion.2
  765.8 56.0 %all-reduce.5.cloned.1.call-done = bf16[384,2048]{1,0:T(8,128)(2,1)} async-done(((bf16[384,2048]{1,0:T(8,128)(2,1)}), bf16[384,2048]{1,0:T(8,128)(2,1)}) %all-reduce.5.cloned.1.call-update) | async-done | bytes 1572880 | tf_op jit(solution)/shard_map/while/body/eval_jaxpr/psum | solution.py:23
  821.9 49.0 %all-reduce.3.cloned.1.call-done = bf16[2048,384]{1,0:T(8,128)(2,1)} async-done(((bf16[2048,384]{1,0:T(8,128)(2,1)}), bf16[2048,384]{1,0:T(8,128)(2,1)}) %all-reduce.3.cloned.1.call-update) | async-done | bytes 1572880 | tf_op jit(solution)/shard_map/while/body/eval_jaxpr/psum | solution.py:21
  870.9 17.0 %select_add_fusion.2 = f32[2048,2048]{1,0:T(8,128)} fusion(f32[2048,2048]{1,0:T(8,128)} %get-tuple-element.276, pred[]{:T(512)S(6)} %compare.21, bf16[2048,384]{1,0:T(8,128)(2,1)} %all-reduce.3.cloned.1.call-done, bf16[384,2048]{1,0:T(8,128)(2,1)} %all-reduce.5.cloned.1.call-done), kind=kOutput, calls=%fused_computation.clone.1 | convolution fusion | flops 3229614080 | bytes 36700160 | tf_op jit(solution)/shard_map/while/body/eval_jaxpr/dot_general | solution.py:24
  887.9 1.3 broadcast_select_fusion.2
  889.3 1.0 copy-done
  890.4 1.4 dynamic-slice_select_fusion.2
  891.9 55.7 %all-reduce.5.cloned.1.call-done = bf16[384,2048]{1,0:T(8,128)(2,1)} async-done(((bf16[384,2048]{1,0:T(8,128)(2,1)}), bf16[384,2048]{1,0:T(8,128)(2,1)}) %all-reduce.5.cloned.1.call-update) | async-done | bytes 1572880 | tf_op jit(solution)/shard_map/while/body/eval_jaxpr/psum | solution.py:23
  947.6 49.0 %all-reduce.3.cloned.1.call-done = bf16[2048,384]{1,0:T(8,128)(2,1)} async-done(((bf16[2048,384]{1,0:T(8,128)(2,1)}), bf16[2048,384]{1,0:T(8,128)(2,1)}) %all-reduce.3.cloned.1.call-update) | async-done | bytes 1572880 | tf_op jit(solution)/shard_map/while/body/eval_jaxpr/psum | solution.py:21
  996.6 17.0 %select_add_fusion.2 = f32[2048,2048]{1,0:T(8,128)} fusion(f32[2048,2048]{1,0:T(8,128)} %get-tuple-element.276, pred[]{:T(512)S(6)} %compare.21, bf16[2048,384]{1,0:T(8,128)(2,1)} %all-reduce.3.cloned.1.call-done, bf16[384,2048]{1,0:T(8,128)(2,1)} %all-reduce.5.cloned.1.call-done), kind=kOutput, calls=%fused_computation.clone.1 | convolution fusion | flops 3229614080 | bytes 36700160 | tf_op jit(solution)/shard_map/while/body/eval_jaxpr/dot_general | solution.py:24
  1013.6 9.0 convert_element_type.3
  (43 shorter events, 2.4 us)
Async XLA Ops:
  6.5 64.0 %all-reduce.5.cloned.1.call-start = ((), (), s32[]{:S(2)}) async-start(), calls=%async_computation.1 | async-start | bytes 3145728 | tf_op jit(solution)/shard_map/while/body/eval_jaxpr/psum | solution.py:23
  6.6 2.5 copy-start
  7.9 111.9 %all-reduce.3.cloned.1.call-start = ((), (), s32[]{:S(2)}) async-start(), calls=%async_computation | async-start | bytes 3145728 | tf_op jit(solution)/shard_map/while/body/eval_jaxpr/psum | solution.py:21
  131.9 60.0 %all-reduce.5.cloned.1.call-start = ((), (), s32[]{:S(2)}) async-start(), calls=%async_computation.1 | async-start | bytes 3145728 | tf_op jit(solution)/shard_map/while/body/eval_jaxpr/psum | solution.py:23
  131.9 3.0 copy-start
  134.8 106.2 %all-reduce.3.cloned.1.call-start = ((), (), s32[]{:S(2)}) async-start(), calls=%async_computation | async-start | bytes 3145728 | tf_op jit(solution)/shard_map/while/body/eval_jaxpr/psum | solution.py:21
  257.9 59.7 %all-reduce.5.cloned.1.call-start = ((), (), s32[]{:S(2)}) async-start(), calls=%async_computation.1 | async-start | bytes 3145728 | tf_op jit(solution)/shard_map/while/body/eval_jaxpr/psum | solution.py:23
  257.9 2.5 copy-start
  259.2 107.4 %all-reduce.3.cloned.1.call-start = ((), (), s32[]{:S(2)}) async-start(), calls=%async_computation | async-start | bytes 3145728 | tf_op jit(solution)/shard_map/while/body/eval_jaxpr/psum | solution.py:21
  383.6 60.0 %all-reduce.5.cloned.1.call-start = ((), (), s32[]{:S(2)}) async-start(), calls=%async_computation.1 | async-start | bytes 3145728 | tf_op jit(solution)/shard_map/while/body/eval_jaxpr/psum | solution.py:23
  383.6 2.5 copy-start
  385.0 107.9 %all-reduce.3.cloned.1.call-start = ((), (), s32[]{:S(2)}) async-start(), calls=%async_computation | async-start | bytes 3145728 | tf_op jit(solution)/shard_map/while/body/eval_jaxpr/psum | solution.py:21
  509.8 60.0 %all-reduce.5.cloned.1.call-start = ((), (), s32[]{:S(2)}) async-start(), calls=%async_computation.1 | async-start | bytes 3145728 | tf_op jit(solution)/shard_map/while/body/eval_jaxpr/psum | solution.py:23
  509.8 2.5 copy-start
  511.1 107.7 %all-reduce.3.cloned.1.call-start = ((), (), s32[]{:S(2)}) async-start(), calls=%async_computation | async-start | bytes 3145728 | tf_op jit(solution)/shard_map/while/body/eval_jaxpr/psum | solution.py:21
  635.8 60.0 %all-reduce.5.cloned.1.call-start = ((), (), s32[]{:S(2)}) async-start(), calls=%async_computation.1 | async-start | bytes 3145728 | tf_op jit(solution)/shard_map/while/body/eval_jaxpr/psum | solution.py:23
  635.8 2.5 copy-start
  637.2 107.7 %all-reduce.3.cloned.1.call-start = ((), (), s32[]{:S(2)}) async-start(), calls=%async_computation | async-start | bytes 3145728 | tf_op jit(solution)/shard_map/while/body/eval_jaxpr/psum | solution.py:21
  761.9 60.0 %all-reduce.5.cloned.1.call-start = ((), (), s32[]{:S(2)}) async-start(), calls=%async_computation.1 | async-start | bytes 3145728 | tf_op jit(solution)/shard_map/while/body/eval_jaxpr/psum | solution.py:23
  761.9 2.5 copy-start
  763.2 107.7 %all-reduce.3.cloned.1.call-start = ((), (), s32[]{:S(2)}) async-start(), calls=%async_computation | async-start | bytes 3145728 | tf_op jit(solution)/shard_map/while/body/eval_jaxpr/psum | solution.py:21
  887.9 59.7 %all-reduce.5.cloned.1.call-start = ((), (), s32[]{:S(2)}) async-start(), calls=%async_computation.1 | async-start | bytes 3145728 | tf_op jit(solution)/shard_map/while/body/eval_jaxpr/psum | solution.py:23
  887.9 2.5 copy-start
  889.2 107.4 %all-reduce.3.cloned.1.call-start = ((), (), s32[]{:S(2)}) async-start(), calls=%async_computation | async-start | bytes 3145728 | tf_op jit(solution)/shard_map/while/body/eval_jaxpr/psum | solution.py:21
Sparse Core Ops, SparseCore 0:
  9.7 60.7 all-reduce.4
  72.9 46.7 all-reduce.2
  135.1 56.7 all-reduce.4
  194.1 46.7 all-reduce.2
  260.8 56.7 all-reduce.4
  319.8 46.7 all-reduce.2
  386.8 56.7 all-reduce.4
  446.0 46.7 all-reduce.2
  513.0 56.7 all-reduce.4
  572.1 46.7 all-reduce.2
  639.0 56.7 all-reduce.4
  698.1 46.7 all-reduce.2
  765.1 56.7 all-reduce.4
  824.1 46.7 all-reduce.2
  890.8 56.7 all-reduce.4
  949.8 46.7 all-reduce.2
where the time goes:
time: 1030 us
  waiting for transfers between devices  845 us (82%)
  matrix products  131 us (13%)
  other arithmetic  32.2 us (3%)
  between operations  13.1 us (1%)
    psum x8, waiting for transfers between devices, update_step(): lax.psum(jnp.where(row_id == k_step // per_row, b_src, jnp.zeros_like(b_s...  451 us
    psum x8, waiting for transfers between devices, update_step(): lax.psum(jnp.where(col_id == k_step // per_col, a_src, jnp.zeros_like(a_s...  393 us
    dot_general x8, matrix products, update_step(): jnp.dot(a_panel, b_panel, preferred_element_type=jnp.float32)  131 us
  transfers between devices with their start and end apart: 16, of which 16 were waited for; matrix products, arithmetic and copies ran while one was open for 1% of the time, Pallas kernels for 0%

commit v1 on v0

v1 whole, which is shorter than its diff:
```python
import functools

import jax
import jax.numpy as jnp
from jax import lax
from jax.experimental import pallas as pl
from jax.experimental.pallas import tpu as pltpu
from jax.sharding import PartitionSpec as P

MESH = pl.DeviceIdType.MESH
PAIRS = 8
TILE_N = 512
FAR_TILE_N = 1024


def gather_multiply(num_rows, num_cols, a_hbm, b_hbm, c_ref, a_all, b_all, acc, la, lb, asend, arecv, fsend, frecv, bsend, brecv, gsend, grecv, psend, precv):
    row, col = lax.axis_index("row"), lax.axis_index("col")
    chip, core = row // 2, row % 2
    num_chips = num_rows // 2
    rows_a = a_hbm.shape[0]
    depth_b, width = b_hbm.shape
    chunk = rows_a // (2 * PAIRS)
    half = depth_b // 2

    up, down = {"col": (col + 1) % num_cols}, {"col": (col + num_cols - 1) % num_cols}
    east, west = {"row": (row + 2) % num_rows}, {"row": (row + num_rows - 2) % num_rows}
    partner = {"row": row + 1 - 2 * core}
    a_dirs, b_dirs = (up, down), (east, west)

    def remote(src, dst, send, recv, device):
        return pltpu.make_async_remote_copy(src_ref=src, dst_ref=dst, send_sem=send, recv_sem=recv, device_id=device, device_id_type=MESH)

    def a_at(slot, piece):
        return a_all.at[slot, pl.ds(pl.multiple_of(piece * chunk, chunk), chunk)]

    def a_own(way, piece):
        return remote(a_at(0, piece), a_at(1 + way, piece), asend.at[way, piece], arecv.at[way, piece], a_dirs[way])

    def a_far(way, piece):
        return remote(a_at(1 + way, piece), a_at(3, piece), fsend.at[piece], frecv.at[piece], a_dirs[way])

    chip_at = (chip, (chip + num_chips - 1) % num_chips, (chip + 1) % num_chips, (chip + 2) % num_chips)

    def b_at(slot, side, part):
        return b_all.at[chip_at[slot], pl.ds(pl.multiple_of(side * depth_b + part * half, half), half)]

    def b_own(way, part):
        piece = b_at(0, core, part)
        return remote(piece, piece, bsend.at[way, part], brecv.at[way, part], b_dirs[way])

    def b_far(way):
        piece = b_at(1 + way, core, way)
        return remote(piece, piece, gsend.at[way], grecv.at[way], b_dirs[way])

    def b_share(slot, part):
        piece = b_at(slot, core, part)
        return remote(piece, piece, psend.at[slot, part], precv.at[slot, part], partner)

    def a_load(piece):
        return pltpu.make_async_copy(a_hbm.at[pl.ds(piece * chunk, chunk)], a_at(0, piece), la.at[piece])

    def b_load(part):
        return pltpu.make_async_copy(b_hbm.at[pl.ds(part * half, half)], b_at(0, core, part), lb.at[part])

    even, odd = range(0, 2 * PAIRS, 2), range(1, 2 * PAIRS, 2)
    b_load(0).start()
    b_load(1).start()
    for piece in range(2 * PAIRS):
        a_load(piece).start()

    barrier = pltpu.get_barrier_semaphore()
    for device in (up, down, east, west, partner):
        pl.semaphore_signal(barrier, inc=1, device_id=device, device_id_type=MESH)
    pl.semaphore_wait(barrier, 5)

    b_load(0).wait()
    b_load(1).wait()
    for part in range(2):
        b_own(0, part).start()
        b_own(1, 1 - part).start()
    for piece in range(2 * PAIRS):
        a_load(piece).wait()
    for first, second in ((even, odd), (odd, even)):
        for plus, minus in zip(first, second):
            a_own(0, plus).start()
            a_own(1, minus).start()
    for part in range(2):
        b_share(0, part).start()

    for way in range(2):
        b_own(way, way).wait_recv()
        b_far(way).start()
        b_share(1 + way, way).start()

    @pl.loop(0, PAIRS)
    def _(pair):
        for way in range(2):
            piece = 2 * pair + way
            a_own(way, piece).wait_recv()
            a_far(way, piece).start()

    for way in range(2):
        b_own(way, 1 - way).wait_recv()
        b_share(1 + way, 1 - way).start()
    for way in range(2):
        b_far(way).wait_recv()
        b_share(3, way).start()
    for slot in range(4):
        for part in range(2):
            b_share(slot, part).wait_recv()

    block_at = (col, (col + num_cols - 1) % num_cols, (col + 1) % num_cols, (col + 2) % num_cols)

    def dot(slot, rows, cols):
        return jnp.dot(a_all[slot, rows, :], b_all[block_at[slot], :, cols], preferred_element_type=jnp.float32)

    @pl.loop(0, PAIRS // 2)
    def _(quad):
        for pair in (2 * quad, 2 * quad + 1):
            for way in range(2):
                a_own(way, 2 * pair + 1 - way).wait_recv()
        rows = pl.ds(pl.multiple_of(quad * 4 * chunk, 4 * chunk), 4 * chunk)

        @pl.loop(0, width // TILE_N)
        def _(tile):
            cols = pl.ds(pl.multiple_of(tile * TILE_N, TILE_N), TILE_N)
            acc[rows, cols] = dot(0, rows, cols) + dot(1, rows, cols) + dot(2, rows, cols)

    @pl.loop(0, PAIRS - 1)
    def _(pair):
        for way in range(2):
            a_far(way, 2 * pair + way).wait_recv()
        rows = pl.ds(pl.multiple_of(pair * 2 * chunk, 2 * chunk), 2 * chunk)

        @pl.loop(0, width // FAR_TILE_N)
        def _(tile):
            cols = pl.ds(pl.multiple_of(tile * FAR_TILE_N, FAR_TILE_N), FAR_TILE_N)
            c_ref[rows, cols] = (acc[rows, cols] + dot(3, rows, cols)).astype(c_ref.dtype)

    for way in range(2):
        a_far(way, 2 * (PAIRS - 1) + way).wait_recv()

    @pl.loop(0, 2 * PAIRS)
    def _(piece):
        for way in range(2):
            a_own(way, piece).wait_send()

    @pl.loop(0, PAIRS)
    def _(pair):
        for way in range(2):
            a_far(way, 2 * pair + way).wait_send()

    for way in range(2):
        for part in range(2):
            b_own(way, part).wait_send()
        b_far(way).wait_send()
    for slot in range(4):
        for part in range(2):
            b_share(slot, part).wait_send()


def finish(num_cols, c_done, a_all, b_all, acc, c_hbm, c_last, sems):
    rows_c = c_hbm.shape[0]
    last = rows_c // PAIRS
    done = pl.ds(0, rows_c - last)
    tail = pl.ds(rows_c - last, last)
    early = pltpu.make_async_copy(c_done.at[done], c_hbm.at[done], sems.at[0])
    early.start()
    block = (lax.axis_index("col") + 2) % num_cols
    c_last[...] = (acc[tail] + jnp.dot(a_all[3, tail, :], b_all[block], preferred_element_type=jnp.float32)).astype(c_last.dtype)
    late = pltpu.make_async_copy(c_last, c_hbm.at[tail], sems.at[1])
    late.start()
    early.wait()
    late.wait()


def solution(mesh):
    num_rows, num_cols = mesh.shape["row"], mesh.shape["col"]

    def local_product(a_blk, b_blk):
        rows, depth = a_blk.shape
        depth_b, width = b_blk.shape
        dma = pltpu.SemaphoreType.DMA
        vmem = pl.BlockSpec(memory_space=pltpu.VMEM)
        hbm = pl.BlockSpec(memory_space=pltpu.HBM)
        far_flops = 2 * rows * width * depth // PAIRS
        gathered = pl.pallas_call(
            functools.partial(gather_multiply, num_rows, num_cols),
            out_shape=(
                pltpu.VMEM((rows, width), jnp.bfloat16),
                pltpu.VMEM((4, rows, depth), jnp.bfloat16),
                pltpu.VMEM((num_rows // 2, 2 * depth_b, width), jnp.bfloat16),
                pltpu.VMEM((rows, width), jnp.float32),
            ),
            in_specs=[hbm] * 2,
            out_specs=(vmem,) * 4,
            scratch_shapes=[
                dma((2 * PAIRS,)),
                dma((2,)),
                dma((2, 2 * PAIRS)),
                dma((2, 2 * PAIRS)),
                dma((2 * PAIRS,)),
                dma((2 * PAIRS,)),
                dma((2, 2)),
                dma((2, 2)),
                dma((2,)),
                dma((2,)),
                dma((4, 2)),
                dma((4, 2)),
            ],
            cost_estimate=pl.CostEstimate(flops=2 * rows * width * depth * num_cols - far_flops, bytes_accessed=2 * (rows * depth + depth_b * width), transcendentals=0),
            compiler_params=pltpu.CompilerParams(collective_id=0, has_side_effects=True, vmem_limit_bytes=8 * 1024 * 1024),
            name="gather_multiply",
        )(a_blk, b_blk)
        return pl.pallas_call(
            functools.partial(finish, num_cols),
            out_shape=jax.ShapeDtypeStruct((rows, width), jnp.bfloat16),
            in_specs=[vmem] * 4,
            out_specs=hbm,
            scratch_shapes=[pltpu.VMEM((rows // PAIRS, width), jnp.bfloat16), dma((2,))],
            cost_estimate=pl.CostEstimate(flops=far_flops, bytes_accessed=2 * rows * width, transcendentals=0),
            compiler_params=pltpu.CompilerParams(vmem_limit_bytes=8 * 1024 * 1024),
            name="finish",
        )(*(pltpu.with_memory_space_constraint(part, pltpu.VMEM) for part in gathered))

    return jax.shard_map(local_product, mesh=mesh, in_specs=(P(("dp", "row"), "col"), P("row", "col")), out_specs=P(("dp", "row"), "col"), check_vma=False)
```

time: 1030 us -> 114 us (0.11)
  waiting for transfers between devices: 845 us -> 0 us
  matrix products: 131 us -> 0 us
  Pallas kernels: 0 us -> 114 us
  other arithmetic: 32.2 us -> 0 us
  between operations: 13.1 us -> 0.01 us
    psum x16 -> x0, waiting for transfers between devices: 844 us -> none  [the longest x8 451 us: update_step(): lax.psum(jnp.where(row_id == k_step // per_row, b_src, jnp.zeros_like(b_s...]
    dot_general x8 -> x0, matrix products: 131 us -> none  [update_step(): jnp.dot(a_panel, b_panel, preferred_element_type=jnp.float32)]
    pallas_call x0 -> x2, Pallas kernels: none -> 114 us  [the longest x1 111 us: local_product(): pl.pallas_call(functools.partial(gather_multiply, num_rows, num_cols), ou...]
    select_n x16 -> x0, other arithmetic: 23.1 us -> none  [the longest x8 11.7 us: update_step(): jnp.where(row_id == k_step // per_row, b_src, jnp.zeros_like(b_src))]
  transfers between devices with their start and end apart: 16 -> 0, of which waited for: 16 -> 0; matrix products, arithmetic and copies ran while one was open for 1% -> 0% of each run, Pallas kernels for 0% -> 0%
where the time goes in v1:
time: 114 us
  Pallas kernels  114 us (100%)
    pallas_call x1, Pallas kernels, local_product(): pl.pallas_call(functools.partial(gather_multiply, num_rows, num_cols), ou...  111 us
    pallas_call x1, Pallas kernels, local_product(): pl.pallas_call(functools.partial(finish, num_cols), out_shape=jax.ShapeDt...  3.4 us

profile of v1, /device:TPU:97, one launch (start us, length us, event | category | flops | bytes accessed | tf_op | source)
XLA Modules:
  0.0 114.4 jit_solution(14842990635058998986)
XLA Ops:
  0.0 111.0 %gather_multiply.1 = (bf16[2048,2048]{1,0:T(8,128)(2,1)S(1)}, bf16[4,2048,768]{2,1,0:T(8,128)(2,1)S(1)}, bf16[4,768,2048]{2,1,0:T(8,128)(2,1)S(1)}, f32[2048,2048]{1,0:T(8,128)S(1)}) custom-call(bf16[2048,768]{1,0:T(8,128)(2,1)} %a_hbm.1, bf16[384,2048]{1,0:T(8,128)(2,1)} %b_hbm.1), custom_call_target="tpu_custom_call" | custom-call | flops 24964497408 | bytes 4718592 | tf_op jit(solution)/shard_map/gather_multiply/pallas_call | solution.py:187
  111.0 3.4 %finish.1 = bf16[2048,2048]{1,0:T(8,128)(2,1)} custom-call(bf16[2048,2048]{1,0:T(8,128)(2,1)S(1)} %get-tuple-element.9.c_done, bf16[4,2048,768]{2,1,0:T(8,128)(2,1)S(1)} %get-tuple-element.10.a_all, bf16[4,768,2048]{2,1,0:T(8,128)(2,1)S(1)} %get-tuple-element.11.b_all, f32[2048,2048]{1,0:T(8,128)S(1)} %get-tuple-element.12.acc), custom_call_target="tpu_custom_call" | custom-call | flops 805306368 | bytes 8388608 | tf_op jit(solution)/shard_map/finish/pallas_call | solution.py:215

commit v2 on v1

v2 whole, which is shorter than its diff:
```python
import functools

import jax
import jax.numpy as jnp
from jax import lax
from jax.experimental import pallas as pl
from jax.experimental.pallas import tpu as pltpu
from jax.sharding import PartitionSpec as P

MESH = pl.DeviceIdType.MESH
BLOCK = 512
PIECE = 256
LAST = 128
TILE_N = 512
FAR_TILE_N = 1024


def own_plan(rows):
    mid = rows // 2
    return (
        ((0, LAST), (LAST, mid - LAST), (mid, mid // 2), (mid + mid // 2, mid // 2)),
        ((rows - LAST, LAST), (mid, mid - LAST), (0, mid // 2), (mid // 2, mid // 2)),
    )


def far_plan(rows):
    mid = rows // 2
    sizes = [PIECE] * (mid // PIECE - 1) + [LAST] * (PIECE // LAST)
    starts = [sum(sizes[:k]) for k in range(len(sizes))]
    return tuple(zip(starts, sizes)), tuple((rows - start - size, size) for start, size in zip(starts, sizes))


def gather_multiply(num_rows, num_cols, a_hbm, b_hbm, c_ref, a_all, b_all, acc, la, lb, asend, arecv, fsend, frecv, bsend, brecv, gsend, grecv, psend, precv, joined, ready, go):
    row, col = lax.axis_index("row"), lax.axis_index("col")
    chip, core = row // 2, row % 2
    num_chips = num_rows // 2
    rows_a = a_hbm.shape[0]
    depth_b, width = b_hbm.shape
    own, far = own_plan(rows_a), far_plan(rows_a)
    pieces = len(far[0])
    half = depth_b // 2

    up, down = {"col": (col + 1) % num_cols}, {"col": (col + num_cols - 1) % num_cols}
    east, west = {"row": (row + 2) % num_rows}, {"row": (row + num_rows - 2) % num_rows}
    partner = {"row": row + 1 - 2 * core}
    a_dirs, b_dirs = (up, down), (east, west)

    def remote(src, dst, send, recv, device):
        return pltpu.make_async_remote_copy(src_ref=src, dst_ref=dst, send_sem=send, recv_sem=recv, device_id=device, device_id_type=MESH)

    def a_at(slot, place):
        return a_all.at[slot, pl.ds(*place)]

    def a_own(way, k):
        return remote(a_at(0, own[way][k]), a_at(1 + way, own[way][k]), asend.at[way, k], arecv.at[way, k], a_dirs[way])

    def a_far(way, k):
        return remote(a_at(1 + way, far[way][k]), a_at(3, far[way][k]), fsend.at[way, k], frecv.at[way, k], a_dirs[way])

    chip_at = (chip, (chip + num_chips - 1) % num_chips, (chip + 1) % num_chips, (chip + 2) % num_chips)

    def b_at(slot, side, part):
        return b_all.at[chip_at[slot], pl.ds(pl.multiple_of(side * depth_b + part * half, half), half)]

    def b_own(way, part):
        piece = b_at(0, core, part)
        return remote(piece, piece, bsend.at[way, part], brecv.at[way, part], b_dirs[way])

    def b_far(way):
        piece = b_at(1 + way, core, way)
        return remote(piece, piece, gsend.at[way], grecv.at[way], b_dirs[way])

    def b_share(slot, part):
        piece = b_at(slot, core, part)
        return remote(piece, piece, psend.at[slot, part], precv.at[slot, part], partner)

    def a_load(way, k):
        return pltpu.make_async_copy(a_hbm.at[pl.ds(*own[way][k])], a_at(0, own[way][k]), la.at[way, k])

    def b_load(part):
        return pltpu.make_async_copy(b_hbm.at[pl.ds(part * half, half)], b_at(0, core, part), lb.at[part])

    for k in range(2):
        for way in range(2):
            a_load(way, k).start()
    b_load(0).start()
    b_load(1).start()

    barrier = pltpu.get_barrier_semaphore()
    hub, after, across, before = range(num_cols)

    def signal(sem, *devices):
        for device in devices:
            pl.semaphore_signal(sem, inc=1, device_id=device, device_id_type=MESH)

    signal(barrier, up, down)

    @pl.when(col == hub)
    def _():
        signal(barrier, east, west, partner)
        pl.semaphore_wait(barrier, 5)

    @pl.when(col != hub)
    def _():
        pl.semaphore_wait(barrier, 2)

    for k in range(4):
        for way in range(2):
            if k < 2:
                a_load(way, k).wait()
            a_own(way, k).start()

    @pl.when(col == hub)
    def _():
        pl.semaphore_wait(joined, 2)
        signal(ready, east, west, partner)
        pl.semaphore_wait(ready, 3)
        signal(go, up, down)

    @pl.when(col == before)
    def _():
        signal(joined, up)
        pl.semaphore_wait(go, 1)

    @pl.when(col == after)
    def _():
        signal(joined, down)
        pl.semaphore_wait(go, 1)
        signal(go, up)

    @pl.when(col == across)
    def _():
        pl.semaphore_wait(go, 1)

    b_load(0).wait()
    b_load(1).wait()
    for part in range(2):
        b_own(0, part).start()
        b_own(1, 1 - part).start()
    for part in range(2):
        b_share(0, part).start()

    for way in range(2):
        b_own(way, way).wait_recv()
        b_far(way).start()
        b_share(1 + way, way).start()

    for way in range(2):
        for k in range(2):
            a_own(way, k).wait_recv()
        for k in range(pieces):
            a_far(way, k).start()

    for way in range(2):
        b_own(way, 1 - way).wait_recv()
        b_share(1 + way, 1 - way).start()
    for way in range(2):
        b_far(way).wait_recv()
        b_share(3, way).start()
    for slot in range(4):
        for part in range(2):
            b_share(slot, part).wait_recv()

    block_at = (col, (col + num_cols - 1) % num_cols, (col + 1) % num_cols, (col + 2) % num_cols)

    def dot(slot, rows, cols):
        return jnp.dot(a_all[slot, rows, :], b_all[block_at[slot], :, cols], preferred_element_type=jnp.float32)

    def near(block):
        rows = pl.ds(pl.multiple_of(block * BLOCK, BLOCK), BLOCK)

        @pl.loop(0, width // TILE_N)
        def _(tile):
            cols = pl.ds(pl.multiple_of(tile * TILE_N, TILE_N), TILE_N)
            acc[rows, cols] = dot(0, rows, cols) + dot(1, rows, cols) + dot(2, rows, cols)

    def away(start, size):
        rows = pl.ds(start, size)

        @pl.loop(0, width // FAR_TILE_N)
        def _(tile):
            cols = pl.ds(pl.multiple_of(tile * FAR_TILE_N, FAR_TILE_N), FAR_TILE_N)
            c_ref[rows, cols] = (acc[rows, cols] + dot(3, rows, cols)).astype(c_ref.dtype)

    blocks = rows_a // BLOCK
    for k in range(2):
        for way in range(2):
            a_own(way, 2 + k).wait_recv()

        @pl.loop(0, blocks // 2)
        def _(turn):
            near(turn * 2 + k)

    for way in range(2):
        for k in range(4):
            a_own(way, k).wait_send()
        for part in range(2):
            b_own(way, part).wait_send()
        b_far(way).wait_send()
    for slot in range(4):
        for part in range(2):
            b_share(slot, part).wait_send()

    for k in range(pieces):
        for way in range(2):
            a_far(way, k).wait_recv()
            if k < pieces - 1:
                away(*far[way][k])
    for k in range(pieces):
        for way in range(2):
            a_far(way, k).wait_send()


def finish(num_cols, c_done, a_all, b_all, acc, c_hbm, c_last, sems):
    rows_c = c_hbm.shape[0]
    mid = rows_c // 2
    tail = pl.ds(mid - LAST, 2 * LAST)
    copies = []
    for k, rows in enumerate((pl.ds(0, mid - LAST), pl.ds(mid + LAST, mid - LAST))):
        copies.append(pltpu.make_async_copy(c_done.at[rows], c_hbm.at[rows], sems.at[k]))
        copies[-1].start()
    block = (lax.axis_index("col") + 2) % num_cols
    c_last[...] = (acc[tail] + jnp.dot(a_all[3, tail, :], b_all[block], preferred_element_type=jnp.float32)).astype(c_last.dtype)
    copies.append(pltpu.make_async_copy(c_last, c_hbm.at[tail], sems.at[2]))
    copies[-1].start()
    for copy in copies:
        copy.wait()


def solution(mesh):
    num_rows, num_cols = mesh.shape["row"], mesh.shape["col"]

    def local_product(a_blk, b_blk):
        rows, depth = a_blk.shape
        depth_b, width = b_blk.shape
        dma = pltpu.SemaphoreType.DMA
        vmem = pl.BlockSpec(memory_space=pltpu.VMEM)
        hbm = pl.BlockSpec(memory_space=pltpu.HBM)
        far_flops = 4 * LAST * width * depth
        pieces = len(far_plan(rows)[0])
        gathered = pl.pallas_call(
            functools.partial(gather_multiply, num_rows, num_cols),
            out_shape=(
                pltpu.VMEM((rows, width), jnp.bfloat16),
                pltpu.VMEM((4, rows, depth), jnp.bfloat16),
                pltpu.VMEM((num_rows // 2, 2 * depth_b, width), jnp.bfloat16),
                pltpu.VMEM((rows, width), jnp.float32),
            ),
            in_specs=[hbm] * 2,
            out_specs=(vmem,) * 4,
            scratch_shapes=[
                dma((2, 2)),
                dma((2,)),
                dma((2, 4)),
                dma((2, 4)),
                dma((2, pieces)),
                dma((2, pieces)),
                dma((2, 2)),
                dma((2, 2)),
                dma((2,)),
                dma((2,)),
                dma((4, 2)),
                dma((4, 2)),
                pltpu.SemaphoreType.REGULAR,
                pltpu.SemaphoreType.REGULAR,
                pltpu.SemaphoreType.REGULAR,
            ],
            cost_estimate=pl.CostEstimate(flops=2 * rows * width * depth * num_cols - far_flops, bytes_accessed=2 * (rows * depth + depth_b * width), transcendentals=0),
            compiler_params=pltpu.CompilerParams(collective_id=0, has_side_effects=True, vmem_limit_bytes=8 * 1024 * 1024),
            name="gather_multiply",
        )(a_blk, b_blk)
        return pl.pallas_call(
            functools.partial(finish, num_cols),
            out_shape=jax.ShapeDtypeStruct((rows, width), jnp.bfloat16),
            in_specs=[vmem] * 4,
            out_specs=hbm,
            scratch_shapes=[pltpu.VMEM((2 * LAST, width), jnp.bfloat16), dma((3,))],
            cost_estimate=pl.CostEstimate(flops=far_flops, bytes_accessed=2 * rows * width, transcendentals=0),
            compiler_params=pltpu.CompilerParams(vmem_limit_bytes=8 * 1024 * 1024),
            name="finish",
        )(*(pltpu.with_memory_space_constraint(part, pltpu.VMEM) for part in gathered))

    return jax.shard_map(local_product, mesh=mesh, in_specs=(P(("dp", "row"), "col"), P("row", "col")), out_specs=P(("dp", "row"), "col"), check_vma=False)
```

time: 114 us -> 112 us (0.982)
  Pallas kernels: 114 us -> 112 us
    pallas_call x1, Pallas kernels: 111 us -> 108 us  [local_product(): pl.pallas_call(functools.partial(gather_multiply, num_rows, num_cols), ou...]
where the time goes in v2:
time: 112 us
  Pallas kernels  112 us (100%)
    pallas_call x1, Pallas kernels, local_product(): pl.pallas_call(functools.partial(gather_multiply, num_rows, num_cols), ou...  108 us
    pallas_call x1, Pallas kernels, local_product(): pl.pallas_call(functools.partial(finish, num_cols), out_shape=jax.ShapeDt...  3.41 us

profile of v2, /device:TPU:97, one launch (start us, length us, event | category | flops | bytes accessed | tf_op | source)
XLA Modules:
  0.0 111.8 jit_solution(8533558925422790175)
XLA Ops:
  0.0 108.4 %gather_multiply.1 = (bf16[2048,2048]{1,0:T(8,128)(2,1)S(1)}, bf16[4,2048,768]{2,1,0:T(8,128)(2,1)S(1)}, bf16[4,768,2048]{2,1,0:T(8,128)(2,1)S(1)}, f32[2048,2048]{1,0:T(8,128)S(1)}) custom-call(bf16[2048,768]{1,0:T(8,128)(2,1)} %a_hbm.1, bf16[384,2048]{1,0:T(8,128)(2,1)} %b_hbm.1), custom_call_target="tpu_custom_call" | custom-call | flops 24964497408 | bytes 4718592 | tf_op jit(solution)/shard_map/gather_multiply/pallas_call | solution.py:241
  108.4 3.4 %finish.1 = bf16[2048,2048]{1,0:T(8,128)(2,1)} custom-call(bf16[2048,2048]{1,0:T(8,128)(2,1)S(1)} %get-tuple-element.9.c_done, bf16[4,2048,768]{2,1,0:T(8,128)(2,1)S(1)} %get-tuple-element.10.a_all, bf16[4,768,2048]{2,1,0:T(8,128)(2,1)S(1)} %get-tuple-element.11.b_all, f32[2048,2048]{1,0:T(8,128)S(1)} %get-tuple-element.12.acc), custom_call_target="tpu_custom_call" | custom-call | flops 805306368 | bytes 8388608 | tf_op jit(solution)/shard_map/finish/pallas_call | solution.py:272

commit v3 on v2

--- a/solution.py
+++ b/solution.py
@@ -11,6 +11,7 @@
 BLOCK = 512
 PIECE = 256
 LAST = 128
+SPARED = (32, 48)
 TILE_N = 512
 FAR_TILE_N = 1024
 
@@ -19,18 +20,20 @@
     mid = rows // 2
     return (
         ((0, LAST), (LAST, mid - LAST), (mid, mid // 2), (mid + mid // 2, mid // 2)),
-        ((rows - LAST, LAST), (mid, mid - LAST), (0, mid // 2), (mid // 2, mid // 2)),
+        ((rows - LAST, LAST), (mid, mid - LAST), (mid // 2, mid // 2), (0, mid // 2)),
     )
 
 
 def far_plan(rows):
     mid = rows // 2
-    sizes = [PIECE] * (mid // PIECE - 1) + [LAST] * (PIECE // LAST)
-    starts = [sum(sizes[:k]) for k in range(len(sizes))]
-    return tuple(zip(starts, sizes)), tuple((rows - start - size, size) for start, size in zip(starts, sizes))
-
-
-def gather_multiply(num_rows, num_cols, a_hbm, b_hbm, c_ref, a_all, b_all, acc, la, lb, asend, arecv, fsend, frecv, bsend, brecv, gsend, grecv, psend, precv, joined, ready, go):
+    plans = []
+    for spared in SPARED:
+        sizes = [PIECE] * (mid // PIECE - 1) + [LAST] * (PIECE // LAST - 1) + [LAST - spared, spared]
+        plans.append([(sum(sizes[:k]), size) for k, size in enumerate(sizes)])
+    return plans[0], [(rows - start - size, size) for start, size in plans[1]]
+
+
+def gather_multiply(num_rows, num_cols, a_hbm, b_hbm, c_ref, a_all, b_all, acc, la, lb, asend, arecv, fsend, frecv, esend, bsend, brecv, gsend, grecv, psend, precv, peer, joined, ready, go):
     row, col = lax.axis_index("row"), lax.axis_index("col")
     chip, core = row // 2, row % 2
     num_chips = num_rows // 2
@@ -57,6 +60,10 @@
     def a_far(way, k):
         return remote(a_at(1 + way, far[way][k]), a_at(3, far[way][k]), fsend.at[way, k], frecv.at[way, k], a_dirs[way])
 
+    def a_extra(way):
+        place = far[1 - way][-1]
+        return remote(a_at(1 + way, place), a_at(3, place), esend.at[way], frecv.at[1 - way, pieces - 1], a_dirs[way])
+
     chip_at = (chip, (chip + num_chips - 1) % num_chips, (chip + 1) % num_chips, (chip + 2) % num_chips)
 
     def b_at(slot, side, part):
@@ -93,22 +100,40 @@
         for device in devices:
             pl.semaphore_signal(sem, inc=1, device_id=device, device_id_type=MESH)
 
-    signal(barrier, up, down)
+    def send_own(way, between):
+        for k in range(2):
+            a_load(way, k).wait()
+            a_own(way, k).start()
+        for k in range(2):
+            a_load(1 - way, k).wait()
+        for k in range(2, 4):
+            a_own(way, k).start()
+        between()
+        for k in range(4):
+            a_own(1 - way, k).start()
+
+    signal(barrier, up)
 
     @pl.when(col == hub)
     def _():
-        signal(barrier, east, west, partner)
-        pl.semaphore_wait(barrier, 5)
-
-    @pl.when(col != hub)
+        signal(barrier, down, east, west, partner)
+
+    @pl.when(jnp.logical_or(col == after, col == across))
+    def _():
+        pl.semaphore_wait(barrier, 1)
+        signal(peer, down)
+        send_own(1, lambda: pl.semaphore_wait(peer, 1))
+
+    @pl.when(col == before)
     def _():
         pl.semaphore_wait(barrier, 2)
-
-    for k in range(4):
-        for way in range(2):
-            if k < 2:
-                a_load(way, k).wait()
-            a_own(way, k).start()
+        signal(peer, down)
+        send_own(0, lambda: None)
+
+    @pl.when(col == hub)
+    def _():
+        pl.semaphore_wait(peer, 1)
+        send_own(0, lambda: pl.semaphore_wait(barrier, 4))
 
     @pl.when(col == hub)
     def _():
@@ -148,7 +173,7 @@
     for way in range(2):
         for k in range(2):
             a_own(way, k).wait_recv()
-        for k in range(pieces):
+        for k in range(pieces - 1):
             a_far(way, k).start()
 
     for way in range(2):
@@ -161,6 +186,28 @@
         for part in range(2):
             b_share(slot, part).wait_recv()
 
+    for way in range(2):
+        a_own(way, 2).wait_recv()
+
+    def spared(act):
+        @pl.when(col != before)
+        def _():
+            act(a_far(0, pieces - 1))
+
+        @pl.when(col != hub)
+        def _():
+            act(a_far(1, pieces - 1))
+
+        @pl.when(col == after)
+        def _():
+            act(a_extra(1))
+
+        @pl.when(col == across)
+        def _():
+            act(a_extra(0))
+
+    spared(lambda copy: copy.start())
+
     block_at = (col, (col + num_cols - 1) % num_cols, (col + 1) % num_cols, (col + 2) % num_cols)
 
     def dot(slot, rows, cols):
@@ -182,14 +229,15 @@
             cols = pl.ds(pl.multiple_of(tile * FAR_TILE_N, FAR_TILE_N), FAR_TILE_N)
             c_ref[rows, cols] = (acc[rows, cols] + dot(3, rows, cols)).astype(c_ref.dtype)
 
-    blocks = rows_a // BLOCK
-    for k in range(2):
-        for way in range(2):
-            a_own(way, 2 + k).wait_recv()
-
-        @pl.loop(0, blocks // 2)
+    quarter = rows_a // (4 * BLOCK)
+    for first, second in ((1, 2), (0, 3)):
+        if first == 0:
+            for way in range(2):
+                a_own(way, 3).wait_recv()
+
+        @pl.loop(0, 2 * quarter)
         def _(turn):
-            near(turn * 2 + k)
+            near(first * quarter + turn % quarter + (turn // quarter) * (second - first) * quarter)
 
     for way in range(2):
         for k in range(4):
@@ -204,11 +252,12 @@
     for k in range(pieces):
         for way in range(2):
             a_far(way, k).wait_recv()
-            if k < pieces - 1:
+            if k < pieces - 2:
                 away(*far[way][k])
-    for k in range(pieces):
+    for k in range(pieces - 1):
         for way in range(2):
             a_far(way, k).wait_send()
+    spared(lambda copy: copy.wait_send())
 
 
 def finish(num_cols, c_done, a_all, b_all, acc, c_hbm, c_last, sems):
@@ -255,12 +304,14 @@
                 dma((2, 4)),
                 dma((2, pieces)),
                 dma((2, pieces)),
+                dma((2,)),
                 dma((2, 2)),
                 dma((2, 2)),
                 dma((2,)),
                 dma((2,)),
                 dma((4, 2)),
                 dma((4, 2)),
+                pltpu.SemaphoreType.REGULAR,
                 pltpu.SemaphoreType.REGULAR,
                 pltpu.SemaphoreType.REGULAR,
                 pltpu.SemaphoreType.REGULAR,

time: 112 us -> 111 us (level)
  no operation moved by 1% of the time
where the time goes in v3:
time: 111 us
  Pallas kernels  111 us (100%)
    pallas_call x1, Pallas kernels, local_product(): pl.pallas_call(functools.partial(gather_multiply, num_rows, num_cols), ou...  107 us
    pallas_call x1, Pallas kernels, local_product(): pl.pallas_call(functools.partial(finish, num_cols), out_shape=jax.ShapeDt...  3.41 us

profile of v3, /device:TPU:97, one launch (start us, length us, event | category | flops | bytes accessed | tf_op | source)
XLA Modules:
  0.0 110.8 jit_solution(2079958126959726150)
XLA Ops:
  0.0 107.4 %gather_multiply.1 = (bf16[2048,2048]{1,0:T(8,128)(2,1)S(1)}, bf16[4,2048,768]{2,1,0:T(8,128)(2,1)S(1)}, bf16[4,768,2048]{2,1,0:T(8,128)(2,1)S(1)}, f32[2048,2048]{1,0:T(8,128)S(1)}) custom-call(bf16[2048,768]{1,0:T(8,128)(2,1)} %a_hbm.1, bf16[384,2048]{1,0:T(8,128)(2,1)} %b_hbm.1), custom_call_target="tpu_custom_call" | custom-call | flops 24964497408 | bytes 4718592 | tf_op jit(solution)/shard_map/gather_multiply/pallas_call | solution.py:290
  107.4 3.4 %finish.1 = bf16[2048,2048]{1,0:T(8,128)(2,1)} custom-call(bf16[2048,2048]{1,0:T(8,128)(2,1)S(1)} %get-tuple-element.9.c_done, bf16[4,2048,768]{2,1,0:T(8,128)(2,1)S(1)} %get-tuple-element.10.a_all, bf16[4,768,2048]{2,1,0:T(8,128)(2,1)S(1)} %get-tuple-element.11.b_all, f32[2048,2048]{1,0:T(8,128)S(1)} %get-tuple-element.12.acc), custom_call_target="tpu_custom_call" | custom-call | flops 805306368 | bytes 8388608 | tf_op jit(solution)/shard_map/finish/pallas_call | solution.py:323

commit v4 on v3

--- a/solution.py
+++ b/solution.py
@@ -11,7 +11,7 @@
 BLOCK = 512
 PIECE = 256
 LAST = 128
-SPARED = (32, 48)
+SPARED = (32, 32)
 TILE_N = 512
 FAR_TILE_N = 1024
 
@@ -55,7 +55,8 @@
         return a_all.at[slot, pl.ds(*place)]
 
     def a_own(way, k):
-        return remote(a_at(0, own[way][k]), a_at(1 + way, own[way][k]), asend.at[way, k], arecv.at[way, k], a_dirs[way])
+        source = a_hbm.at[pl.ds(*own[way][0])] if k == 0 else a_at(0, own[way][k])
+        return remote(source, a_at(1 + way, own[way][k]), asend.at[way, k], arecv.at[way, k], a_dirs[way])
 
     def a_far(way, k):
         return remote(a_at(1 + way, far[way][k]), a_at(3, far[way][k]), fsend.at[way, k], frecv.at[way, k], a_dirs[way])
@@ -87,12 +88,6 @@
     def b_load(part):
         return pltpu.make_async_copy(b_hbm.at[pl.ds(part * half, half)], b_at(0, core, part), lb.at[part])
 
-    for k in range(2):
-        for way in range(2):
-            a_load(way, k).start()
-    b_load(0).start()
-    b_load(1).start()
-
     barrier = pltpu.get_barrier_semaphore()
     hub, after, across, before = range(num_cols)
 
@@ -101,9 +96,10 @@
             pl.semaphore_signal(sem, inc=1, device_id=device, device_id_type=MESH)
 
     def send_own(way, between):
+        a_own(way, 0).start()
         for k in range(2):
             a_load(way, k).wait()
-            a_own(way, k).start()
+        a_own(way, 1).start()
         for k in range(2):
             a_load(1 - way, k).wait()
         for k in range(2, 4):
@@ -118,6 +114,10 @@
     def _():
         signal(barrier, down, east, west, partner)
 
+    for k in range(2):
+        for way in range(2):
+            a_load(way, k).start()
+
     @pl.when(jnp.logical_or(col == after, col == across))
     def _():
         pl.semaphore_wait(barrier, 1)
@@ -134,6 +134,9 @@
     def _():
         pl.semaphore_wait(peer, 1)
         send_own(0, lambda: pl.semaphore_wait(barrier, 4))
+
+    b_load(0).start()
+    b_load(1).start()
 
     @pl.when(col == hub)
     def _():
@@ -267,7 +270,7 @@
     copies = []
     for k, rows in enumerate((pl.ds(0, mid - LAST), pl.ds(mid + LAST, mid - LAST))):
         copies.append(pltpu.make_async_copy(c_done.at[rows], c_hbm.at[rows], sems.at[k]))
-        copies[-1].start()
+        copies[-1].start(priority=k)
     block = (lax.axis_index("col") + 2) % num_cols
     c_last[...] = (acc[tail] + jnp.dot(a_all[3, tail, :], b_all[block], preferred_element_type=jnp.float32)).astype(c_last.dtype)
     copies.append(pltpu.make_async_copy(c_last, c_hbm.at[tail], sems.at[2]))

time: 111 us -> 110 us (level)
    pallas_call x1, Pallas kernels: 107 us -> 106 us  [local_product(): pl.pallas_call(functools.partial(gather_multiply, num_rows, num_cols), ou...]
where the time goes in v4:
time: 110 us
  Pallas kernels  110 us (100%)
    pallas_call x1, Pallas kernels, local_product(): pl.pallas_call(functools.partial(gather_multiply, num_rows, num_cols), ou...  106 us
    pallas_call x1, Pallas kernels, local_product(): pl.pallas_call(functools.partial(finish, num_cols), out_shape=jax.ShapeDt...  3.39 us

profile of v4, /device:TPU:97, one launch (start us, length us, event | category | flops | bytes accessed | tf_op | source)
XLA Modules:
  0.0 109.7 jit_solution(15908660990142213250)
XLA Ops:
  0.0 106.3 %gather_multiply.1 = (bf16[2048,2048]{1,0:T(8,128)(2,1)S(1)}, bf16[4,2048,768]{2,1,0:T(8,128)(2,1)S(1)}, bf16[4,768,2048]{2,1,0:T(8,128)(2,1)S(1)}, f32[2048,2048]{1,0:T(8,128)S(1)}) custom-call(bf16[2048,768]{1,0:T(8,128)(2,1)} %a_hbm.1, bf16[384,2048]{1,0:T(8,128)(2,1)} %b_hbm.1), custom_call_target="tpu_custom_call" | custom-call | flops 24964497408 | bytes 4718592 | tf_op jit(solution)/shard_map/gather_multiply/pallas_call | solution.py:293
  106.3 3.4 %finish.1 = bf16[2048,2048]{1,0:T(8,128)(2,1)} custom-call(bf16[2048,2048]{1,0:T(8,128)(2,1)S(1)} %get-tuple-element.9.c_done, bf16[4,2048,768]{2,1,0:T(8,128)(2,1)S(1)} %get-tuple-element.10.a_all, bf16[4,768,2048]{2,1,0:T(8,128)(2,1)S(1)} %get-tuple-element.11.b_all, f32[2048,2048]{1,0:T(8,128)S(1)} %get-tuple-element.12.acc), custom_call_target="tpu_custom_call" | custom-call | flops 805306368 | bytes 8388608 | tf_op jit(solution)/shard_map/finish/pallas_call | solution.py:326

commit v5 on v4

--- a/solution.py
+++ b/solution.py
@@ -11,7 +11,7 @@
 BLOCK = 512
 PIECE = 256
 LAST = 128
-SPARED = (32, 32)
+SPARED = (40, 32)
 TILE_N = 512
 FAR_TILE_N = 1024
 
@@ -95,8 +95,10 @@
         for device in devices:
             pl.semaphore_signal(sem, inc=1, device_id=device, device_id_type=MESH)
 
-    def send_own(way, between):
+    def send_own(way, between=None):
         a_own(way, 0).start()
+        if between is None:
+            a_own(1 - way, 0).start()
         for k in range(2):
             a_load(way, k).wait()
         a_own(way, 1).start()
@@ -104,8 +106,10 @@
             a_load(1 - way, k).wait()
         for k in range(2, 4):
             a_own(way, k).start()
-        between()
-        for k in range(4):
+        if between is not None:
+            between()
+            a_own(1 - way, 0).start()
+        for k in range(1, 4):
             a_own(1 - way, k).start()
 
     signal(barrier, up)
@@ -128,7 +132,7 @@
     def _():
         pl.semaphore_wait(barrier, 2)
         signal(peer, down)
-        send_own(0, lambda: None)
+        send_own(0)
 
     @pl.when(col == hub)
     def _():

time: 110 us -> 110 us (level)
  no operation moved by 1% of the time
where the time goes in v5:
time: 110 us; the launch traced here: 109 us
  Pallas kernels  109 us (99%)
    pallas_call x1, Pallas kernels, local_product(): pl.pallas_call(functools.partial(gather_multiply, num_rows, num_cols), ou...  106 us
    pallas_call x1, Pallas kernels, local_product(): pl.pallas_call(functools.partial(finish, num_cols), out_shape=jax.ShapeDt...  3.39 us

profile of v5, /device:TPU:97, one launch (start us, length us, event | category | flops | bytes accessed | tf_op | source)
XLA Modules:
  0.0 109.4 jit_solution(18326726279407284269)
XLA Ops:
  0.0 106.0 %gather_multiply.1 = (bf16[2048,2048]{1,0:T(8,128)(2,1)S(1)}, bf16[4,2048,768]{2,1,0:T(8,128)(2,1)S(1)}, bf16[4,768,2048]{2,1,0:T(8,128)(2,1)S(1)}, f32[2048,2048]{1,0:T(8,128)S(1)}) custom-call(bf16[2048,768]{1,0:T(8,128)(2,1)} %a_hbm.1, bf16[384,2048]{1,0:T(8,128)(2,1)} %b_hbm.1), custom_call_target="tpu_custom_call" | custom-call | flops 24964497408 | bytes 4718592 | tf_op jit(solution)/shard_map/gather_multiply/pallas_call | solution.py:297
  106.0 3.4 %finish.1 = bf16[2048,2048]{1,0:T(8,128)(2,1)} custom-call(bf16[2048,2048]{1,0:T(8,128)(2,1)S(1)} %get-tuple-element.9.c_done, bf16[4,2048,768]{2,1,0:T(8,128)(2,1)S(1)} %get-tuple-element.10.a_all, bf16[4,768,2048]{2,1,0:T(8,128)(2,1)S(1)} %get-tuple-element.11.b_all, f32[2048,2048]{1,0:T(8,128)S(1)} %get-tuple-element.12.acc), custom_call_target="tpu_custom_call" | custom-call | flops 805306368 | bytes 8388608 | tf_op jit(solution)/shard_map/finish/pallas_call | solution.py:330
